TPU v7x, 32 devices: a whole 2x2x4 slice. The times are simulated.
32 devices in a mesh: pairs: 16 (over z, y, x), comp: 2 (over core).
Axes of the slice: x: 2, y: 2, z: 4, core: 2. Of those that a mesh axis runs over, the one named last changes fastest.
Arguments:
- effects: float32 [49, 131072], P(None, 'pairs'), may hold values from -24 to 24
- se_table: float32 [16, 49], replicated, may hold values from 0.5 to 2
- se_index: int32 [256], P('pairs'), may hold values from 0 to 15
- base_root: float32 [16, 49, 49], replicated, may hold values from -0.875 to 0.875
- grid_scale: float32 [16], replicated, may hold values from 0.25 to 4
- comp_base: int32 [256], P('comp'), may hold values from 0 to 15
- comp_grid: int32 [256], P('comp'), may hold values from 0 to 15
- weights: float32 [256], P('comp'), may hold values from 0.2 to 5
Outputs:
- responsibility: float32 [256, 131072], P('comp', 'pairs')
- log_weights: float32 [256], P('comp')
- pair_loglik: float32 [131072], P('pairs')
All inputs are finite; a program needn't handle non-finite values.
Results may differ from a plain program's by a relative error of at most 0.0003.
Values sent between devices are 32-bit elements; how exact they have to be, the bound alone decides.
A program may use at most 384 MiB of HBM per device.

v0:
```python
import math

import jax
import jax.numpy as jnp
from jax import lax
from jax.sharding import PartitionSpec as P

TILE = 512


def joined(part, axis, combine):
    gathered = jax.tree.map(lambda a: lax.all_gather(a, axis), part)

    def take(source):
        return jax.tree.map(lambda a: lax.dynamic_index_in_dim(a, source, 0, False), gathered)

    return lax.fori_loop(
        1, lax.axis_size(axis), lambda source, state: combine(state, take(source)), take(0)
    )


def build_factors(se_rows, covar_rows, scale_rows):
    tissues = se_rows.shape[1]
    identity = jnp.eye(tissues, dtype=jnp.float32)
    system = (scale_rows * scale_rows)[:, None, None] * covar_rows.reshape(-1, tissues, tissues)
    system = system + identity[None] * (se_rows * se_rows)[:, :, None]
    factor = jnp.linalg.cholesky(system)
    eye_full = jnp.broadcast_to(identity, factor.shape)
    inverse = jax.scipy.linalg.solve_triangular(factor, eye_full, lower=True)
    logdet = jnp.sum(jnp.log(jnp.diagonal(factor, axis1=1, axis2=2)), axis=1)
    return (inverse, logdet)


def exact_dot(left, right):
    return jnp.dot(left, right, precision=lax.Precision.HIGHEST, preferred_element_type=jnp.float32)


def per_device(effects, se_table, se_index, base_root, grid_scale, comp_base, comp_grid, weights):
    tissues = effects.shape[0]
    local_pairs = effects.shape[1]
    comp_count = comp_base.shape[0]
    block_count = se_table.shape[0]
    covariances = jnp.einsum("uij,ukj->uik", base_root, base_root, precision=lax.Precision.HIGHEST)
    covariances = covariances.reshape(covariances.shape[0], tissues * tissues)
    base_pick = (
        comp_base[:, None] == jnp.arange(covariances.shape[0], dtype=jnp.int32)[None]
    ).astype(jnp.float32)
    comp_covar = exact_dot(base_pick, covariances)
    grid_pick = (
        comp_grid[:, None] == jnp.arange(grid_scale.shape[0], dtype=jnp.int32)[None]
    ).astype(jnp.float32)
    comp_scale = exact_dot(grid_pick, grid_scale)
    item_share = block_count * comp_count // lax.axis_size("pairs")
    item_first = lax.axis_index("pairs") * item_share
    item_ids = item_first + jnp.arange(item_share, dtype=jnp.int32)
    block_pick = (
        (item_ids // comp_count)[:, None] == jnp.arange(block_count, dtype=jnp.int32)[None]
    ).astype(jnp.float32)
    item_pick = (
        (item_ids % comp_count)[:, None] == jnp.arange(comp_count, dtype=jnp.int32)[None]
    ).astype(jnp.float32)
    own_inverse, own_logdet = build_factors(
        exact_dot(block_pick, se_table),
        exact_dot(item_pick, comp_covar),
        exact_dot(item_pick, comp_scale),
    )
    inverse, logdet = (
        lax.all_gather(own_inverse, "pairs", axis=0, tiled=True),
        lax.all_gather(own_logdet, "pairs", axis=0, tiled=True),
    )
    whiten_table = inverse.reshape(block_count, comp_count, tissues, tissues).transpose(0, 3, 2, 1)
    whiten_table = whiten_table.reshape(block_count, tissues, tissues * comp_count)
    logdet_table = logdet.reshape(block_count, comp_count)
    log_prior = jnp.log(weights)
    constant = 0.5 * tissues * math.log(2.0 * math.pi)

    def one_tile(tile_id, scores):
        block_id = se_index[tile_id]
        block_table = lax.dynamic_index_in_dim(whiten_table, block_id, 0, keepdims=False)
        tile_data = lax.dynamic_slice_in_dim(effects, tile_id * TILE, TILE, 1)
        whitened = lax.dot_general(
            block_table,
            tile_data,
            (((0,), (0,)), ((), ())),
            precision=lax.Precision.HIGHEST,
            preferred_element_type=jnp.float32,
        )
        whitened = whitened.reshape(tissues, comp_count, TILE)
        quadratic = jnp.sum(whitened * whitened, axis=0)
        logdet_row = lax.dynamic_index_in_dim(logdet_table, block_id, 0, keepdims=False)
        tile_scores = log_prior[:, None] - 0.5 * quadratic - logdet_row[:, None] - constant
        return lax.dynamic_update_slice_in_dim(scores, tile_scores, tile_id * TILE, 1)

    scores = lax.fori_loop(
        0, local_pairs // TILE, one_tile, jnp.zeros((comp_count, local_pairs), jnp.float32)
    )
    local_max = jnp.max(scores, axis=0)
    local_sum = jnp.sum(jnp.exp(scores - local_max), axis=0)

    def combine(former, latter):
        larger = jnp.maximum(former[0], latter[0])
        return (
            larger,
            former[1] * jnp.exp(former[0] - larger) + latter[1] * jnp.exp(latter[0] - larger),
        )

    score_max, score_sum = joined((local_max, local_sum), "comp", combine)
    pair_loglik = score_max + jnp.log(score_sum)
    responsibility = jnp.exp(scores - pair_loglik)
    masses = lax.psum(jnp.sum(responsibility, axis=1), "pairs")
    all_pairs = local_pairs * lax.axis_size("pairs")
    all_comps = comp_count * lax.axis_size("comp")
    log_weights = jnp.log((masses + 1.0) / (all_pairs + all_comps))
    return (responsibility, log_weights, pair_loglik)


def solution(mesh):
    placed = (P(None, "pairs"), P(), P("pairs"), P(), P(), P("comp"), P("comp"), P("comp"))
    return jax.shard_map(
        per_device,
        mesh=mesh,
        in_specs=placed,
        out_specs=(P("comp", "pairs"), P("comp"), P("pairs")),
        check_vma=False,
    )
```

profile of v0, /device:TPU:0, one launch (start us, length us, event | category | flops | bytes accessed | tf_op | source)
XLA Modules:
  0.0 1578.0 jit_solution(9261916296940407890)
XLA Ops:
  35.2 576.8 %custom-call.8 = f32[128,49,49]{2,1,0:T(8,128)} custom-call(f32[128,49,49]{2,1,0:T(8,128)} %fusion.5), custom_call_target="Cholesky" | custom-call | tf_op jit(solution)/shard_map/jit(cholesky)/cholesky | solution.py:27
  618.5 37.6 %custom-call.9 = f32[128,1,49,49]{0,2,3,1:T(8,128)S(1)} custom-call(f32[128,1,49,49]{0,3,2,1:T(8,128)} %get-tuple-element.235), custom_call_target="InvertDiagBlocksLowerTriangular" | custom-call | tf_op jit(solution)/shard_map/jit(_solve_triangular)/vmap()/triangular_solve | solution.py:29
  675.0 59.4 %all-gather.2 = f32[16,1,128]{2,1,0:T(1,128)S(1)} all-gather(f32[1,1,128]{2,1,0:T(1,128)S(1)} %bitcast.70), channel_id=1, replica_groups=mesh['pairs'=16,'comp'=2] {'pairs'}, dimensions={0}, use_global_device_ids=true | all-gather | bytes 8704 | tf_op jit(solution)/shard_map/all_gather | solution.py:69
  734.4 403.9 %all-gather.5.cloned.1.call-done = f32[2048,49,49]{0,2,1:T(8,128)} async-done(((f32[128,49,49]{0,2,1:T(8,128)}), f32[2048,49,49]{0,2,1:T(8,128)}) %all-gather.5.cloned.1.call-update) | async-done | bytes 19669008 | tf_op jit(solution)/shard_map/all_gather | solution.py:68
  1138.3 21.0 %reshape.91 = f32[16,128,49,49]{1,0,3,2:T(8,128)} reshape(f32[2048,49,49]{0,2,1:T(8,128)} %all-gather.5.cloned.1.call-done) | data formatting | bytes 39337984 | tf_op jit(solution)/shard_map/reshape | solution.py:71
  1159.2 21.0 %copy.72 = f32[16,128,49,49]{1,2,0,3:T(8,128)} copy(f32[16,128,49,49]{1,0,3,2:T(8,128)} %reshape.91) | data formatting | bytes 39337984 | tf_op jit(solution)/shard_map/reshape | solution.py:71
  1180.2 22.4 %reshape.92 = f32[16,49,6272]{2,0,1:T(8,128)} reshape(f32[16,49,49,128]{3,2,0,1:T(8,128)} %bitcast.62) | data formatting | bytes 39337984 | tf_op jit(solution)/shard_map/reshape | solution.py:72
  1205.1 313.8 %while.10 = (s32[]{:T(128)}, f32[128,8192]{1,0:T(8,128)}, f32[128]{0:T(128)S(1)}, s32[16]{0:T(128)S(1)}, f32[16,49,6272]{2,0,1:T(8,128)}, /*index=5*/f32[49,8192...) while((s32[]{:T(128)}, f32[128,8192]{1,0:T(8,128)}, ...), condition=%wide.region_5.6_spmd, body=%wide.region_3.5_spmd.sunk | while | flops 1894842368 | bytes 9508585 | solution.py:94
  1232.2 11.3 multiply_reduce_fusion.2
  1251.8 11.3 multiply_reduce_fusion.2
  1271.4 11.3 multiply_reduce_fusion.2
  1291.0 11.3 multiply_reduce_fusion.2
  1310.6 11.3 multiply_reduce_fusion.2
  1330.3 11.3 multiply_reduce_fusion.2
  1349.9 11.3 multiply_reduce_fusion.2
  1369.5 11.3 multiply_reduce_fusion.2
  1389.1 11.3 multiply_reduce_fusion.2
  1408.7 11.3 multiply_reduce_fusion.2
  1428.3 11.3 multiply_reduce_fusion.2
  1447.9 11.3 multiply_reduce_fusion.2
  1467.5 11.3 multiply_reduce_fusion.2
  1487.2 11.3 multiply_reduce_fusion.2
  1506.8 11.3 multiply_reduce_fusion.2
  1531.3 39.3 %psum.7 = f32[128]{0:T(128)S(1)} all-reduce(f32[128]{0:T(128)S(1)} %get-tuple-element.233), channel_id=1, replica_groups=mesh['pairs'=16,'comp'=2] {'pairs'}, use_global_device_ids=true, to_apply=%region_9.10 | all-reduce | flops 128 | bytes 1024 | tf_op jit(solution)/shard_map/psum | solution.py:110
  (147 shorter events, 181.6 us)
Async XLA Ops:
  7.2 0.7 copy-start
  7.2 1131.1 %all-gather.5.cloned.1.call-start = ((), (), s32[]{:S(2)}) async-start(), calls=%async_computation | async-start | bytes 23883776 | tf_op jit(solution)/shard_map/all_gather | solution.py:68
  669.3 4.6 copy-start.3
  1202.6 2.5 copy-start.4
  1521.3 7.5 copy-start.2
  1528.8 42.4 %copy-start.1 = (f32[16,49]{1,0:T(8,128)S(1)}, f32[16,49]{1,0:T(8,128)}, u32[]{:S(2)}) copy-start(f32[16,49]{1,0:T(8,128)} %param.11) | copy-start | bytes 9412
Sparse Core Ops, SparseCore 0:
  674.0 464.2 all-gather.4
where the time goes:
time: 1580 us
  other arithmetic  649 us (41%)
  waiting for transfers between devices  404 us (26%)
  matrix products  196 us (12%)
  local copies, waits for them, and re-layouts  181 us (11%)
  blocking collectives  102 us (6%)
  loops' own time  31.6 us (2%)
    another operation x4, other arithmetic, build_factors(): factor = jnp.linalg.cholesky(system)  577 us
    all_gather x1, waiting for transfers between devices, per_device(): lax.all_gather(own_inverse, 'pairs', axis=0, tiled=True)  404 us
    dot_general x16, matrix products, one_tile(): lax.dot_general(block_table, tile_data, (((0,), (0,)), ((), ())), precisi...  181 us
    dynamic_slice x32, local copies, waits for them, and re-layouts, one_tile(): lax.dynamic_index_in_dim(whiten_table, block_id, 0, keepdims=False)  76 us
    all_gather x1, blocking collectives, per_device(): lax.all_gather(own_logdet, 'pairs', axis=0, tiled=True)  59.4 us
    reshape x2, local copies, waits for them, and re-layouts, per_device(): inverse.reshape(block_count, comp_count, tissues, tissues)  42 us
    psum x1, blocking collectives, per_device(): masses = lax.psum(jnp.sum(responsibility, axis=1), 'pairs')  39.3 us
    another operation x3, other arithmetic, build_factors(): inverse = jax.scipy.linalg.solve_triangular(factor, eye_full, lower=True)  39.1 us
  transfers between devices with their start and end apart: 1, of which 1 were waited for; matrix products, arithmetic and copies ran while one was open for 0% of the time, Pallas kernels for 0%

commit v1 on v0

v1 whole, which is shorter than its diff:
```python
import math

import jax
import jax.numpy as jnp
from jax import lax
from jax.experimental import pallas as pl
from jax.experimental.pallas import tpu as pltpu
from jax.sharding import PartitionSpec as P

SUB = 8


def exact_dot(left, right):
    return jnp.dot(left, right, precision=lax.Precision.HIGHEST, preferred_element_type=jnp.float32)


def split_terms(value):
    high = value.astype(jnp.bfloat16)
    return high, (value - high.astype(jnp.float32)).astype(jnp.bfloat16)


def factor_pattern(pattern, se_square, covar, upper, inverse, table, prior, bias, tissues, constant):
    blocks = -(-tissues // SUB)
    comps = covar.shape[2]
    slot = table.shape[1] // 4
    sub_iota = lax.broadcasted_iota(jnp.int32, (SUB, comps), 0)
    half_logdet = jnp.zeros((1, comps), jnp.float32)
    for first in range(0, tissues, 4):
        row_block = first // SUB
        rows = range(first, min(first + 4, tissues))
        system, solved = {}, {}
        for row in rows:
            system[row] = [covar[row, v * SUB : (v + 1) * SUB, :] for v in range(row_block, blocks)]
            on_diag = sub_iota == row % SUB
            system[row][0] = system[row][0] + jnp.where(on_diag, se_square[pattern, row], 0.0)
            solved[row] = [jnp.zeros((SUB, comps), jnp.float32) for _ in range(row_block)]
            solved[row].append(jnp.where(on_diag, 1.0, 0.0))
        for col in range(first):
            col_block = col // SUB
            up = [upper[col, v * SUB : (v + 1) * SUB, :] for v in range(row_block, blocks)]
            inv = [inverse[col, v * SUB : (v + 1) * SUB, :] for v in range(col_block + 1)]
            for row in rows:
                mult = upper[col, row : row + 1, :]
                for n, part in enumerate(up):
                    system[row][n] = system[row][n] - mult * part
                for n, part in enumerate(inv):
                    solved[row][n] = solved[row][n] - mult * part
        for row in rows:
            pivot = system[row][0][row % SUB : row % SUB + 1, :]
            root = lax.rsqrt(pivot)
            root = root * (1.5 - 0.5 * pivot * root * root)
            half_logdet = half_logdet + 0.5 * jnp.log(pivot)
            up = [part * root for part in system[row]]
            inv = [part * root for part in solved[row]]
            for n, part in enumerate(up):
                upper[row, (row_block + n) * SUB : (row_block + n + 1) * SUB, :] = part
            for n, part in enumerate(inv):
                inverse[row, n * SUB : (n + 1) * SUB, :] = part
            for later in rows:
                if later > row:
                    mult = up[0][later % SUB : later % SUB + 1, :]
                    for n, part in enumerate(up):
                        system[later][n] = system[later][n] - mult * part
                    for n, part in enumerate(inv):
                        solved[later][n] = solved[later][n] - mult * part
            if len(inv) % 2:
                inv = inv + [jnp.zeros((SUB, comps), jnp.float32)]
            high, low = split_terms(jnp.concatenate(inv, axis=0))
            lanes = slice((row % 2) * comps, (row % 2 + 1) * comps)
            height = len(inv) * SUB
            table[row // 2, 0:height, lanes] = high
            table[row // 2, slot : slot + height, lanes] = high
            table[row // 2, 2 * slot : 2 * slot + height, lanes] = low
            table[row // 2, 3 * slot : 3 * slot + height, lanes] = low
    bias[...] = jnp.log(prior[...]) - half_logdet - constant


def make_body(tissues):
    constant = 0.5 * tissues * math.log(2.0 * math.pi)

    def body(order, patterns, se_square, effects, covar, prior, scores, peak, total,
             upper, inverse, table, bias, quad, wide):
        step = pl.program_id(0)
        slot = table.shape[1] // 4
        comps = covar.shape[2]

        @pl.when(step == 0)
        def _():
            table[...] = jnp.zeros(table.shape, table.dtype)
            wide[...] = jnp.zeros(wide.shape, wide.dtype)

        fresh = jnp.logical_or(
            step == 0, patterns[step] != patterns[jnp.maximum(step - 1, 0)]
        )

        @pl.when(fresh)
        def _():
            factor_pattern(patterns[step], se_square, covar, upper, inverse, table, prior, bias,
                           tissues, constant)

        tile = effects[...]
        high = tile.astype(jnp.bfloat16).astype(jnp.float32)
        wide[0:tissues, :] = high
        wide[slot : slot + tissues, :] = tile - high
        turned = wide[...].T.astype(jnp.bfloat16)
        packed = jnp.concatenate([turned, turned], axis=1)
        quad[...] = jnp.zeros(quad.shape, quad.dtype)

        def pair_of_rows(index, carry):
            white = jnp.dot(packed, table[index], preferred_element_type=jnp.float32)
            white = white * white
            quad[...] += white[:, :comps] + white[:, comps:]
            return carry

        lax.fori_loop(0, table.shape[0], pair_of_rows, 0)
        found = (bias[...] - 0.5 * quad[...]).T
        scores[...] = found
        top = jnp.max(found, axis=0, keepdims=True)
        peak[...] = top
        total[...] = jnp.sum(jnp.exp(found - top), axis=0, keepdims=True)

    return body


def score_tiles(effects, se_table, se_index, covar, weights):
    tissues, pairs = effects.shape
    tiles = se_index.shape[0]
    comps = weights.shape[0]
    width = pairs // tiles
    padded = covar.shape[1]
    slot = 16 * (-(-tissues // 16))
    place = jnp.arange(tiles, dtype=jnp.int32)
    before = (se_index[None, :] < se_index[:, None]) | (
        (se_index[None, :] == se_index[:, None]) & (place[None, :] < place[:, None])
    )
    rank = jnp.sum(before.astype(jnp.int32), axis=1)
    hit = rank[None, :] == place[:, None]
    order = jnp.sum(jnp.where(hit, place[None, :], 0), axis=1)
    patterns = jnp.sum(jnp.where(hit, se_index[None, :], 0), axis=1)
    grid_spec = pltpu.PrefetchScalarGridSpec(
        num_scalar_prefetch=3,
        grid=(tiles,),
        in_specs=[
            pl.BlockSpec((tissues, width), lambda t, order, *_: (0, order[t])),
            pl.BlockSpec(covar.shape, lambda t, *_: (0, 0, 0)),
            pl.BlockSpec((1, comps), lambda t, *_: (0, 0)),
        ],
        out_specs=[
            pl.BlockSpec((comps, width), lambda t, order, *_: (0, order[t])),
            pl.BlockSpec((1, width), lambda t, order, *_: (0, order[t])),
            pl.BlockSpec((1, width), lambda t, order, *_: (0, order[t])),
        ],
        scratch_shapes=[
            pltpu.VMEM((tissues, padded, comps), jnp.float32),
            pltpu.VMEM((tissues, padded, comps), jnp.float32),
            pltpu.VMEM(((tissues + 1) // 2, 4 * slot, 2 * comps), jnp.bfloat16),
            pltpu.VMEM((1, comps), jnp.float32),
            pltpu.VMEM((width, comps), jnp.float32),
            pltpu.VMEM((2 * slot, width), jnp.float32),
        ],
    )
    return pl.pallas_call(
        make_body(tissues),
        grid_spec=grid_spec,
        out_shape=[
            jax.ShapeDtypeStruct((comps, pairs), jnp.float32),
            jax.ShapeDtypeStruct((1, pairs), jnp.float32),
            jax.ShapeDtypeStruct((1, pairs), jnp.float32),
        ],
        compiler_params=pltpu.CompilerParams(
            dimension_semantics=("arbitrary",), vmem_limit_bytes=48 * 1024 * 1024
        ),
        name="score_tiles",
    )(order, patterns, se_table * se_table, effects, covar, weights[None])


def per_device(effects, se_table, se_index, base_root, grid_scale, comp_base, comp_grid, weights):
    tissues = effects.shape[0]
    comps = comp_base.shape[0]
    padded = SUB * (-(-tissues // SUB))
    right = jnp.pad(base_root, ((0, 0), (0, padded - tissues), (0, 0)))
    covariances = jnp.einsum("uij,ukj->uik", base_root, right, precision=lax.Precision.HIGHEST)
    base_pick = (
        jnp.arange(covariances.shape[0], dtype=jnp.int32)[:, None] == comp_base[None]
    ).astype(jnp.float32)
    grid_pick = (
        comp_grid[:, None] == jnp.arange(grid_scale.shape[0], dtype=jnp.int32)[None]
    )
    comp_scale = jnp.sum(jnp.where(grid_pick, grid_scale[None], 0.0), axis=1)
    covar = lax.dot_general(
        covariances.reshape(covariances.shape[0], tissues * padded),
        base_pick,
        (((0,), (0,)), ((), ())),
        precision=lax.Precision.HIGHEST,
        preferred_element_type=jnp.float32,
    )
    covar = (covar * (comp_scale * comp_scale)[None]).reshape(tissues, padded, comps)
    scores, peak, total = score_tiles(effects, se_table, se_index, covar, weights)
    part = jnp.concatenate([peak, total], axis=0)
    every = lax.all_gather(part, "comp")
    score_max = jnp.max(every[:, 0], axis=0)
    score_sum = jnp.sum(every[:, 1] * jnp.exp(every[:, 0] - score_max[None]), axis=0)
    pair_loglik = score_max + jnp.log(score_sum)
    responsibility = jnp.exp(scores - pair_loglik)
    masses = lax.psum(jnp.sum(responsibility, axis=1), "pairs")
    all_pairs = effects.shape[1] * lax.axis_size("pairs")
    all_comps = comps * lax.axis_size("comp")
    log_weights = jnp.log((masses + 1.0) / (all_pairs + all_comps))
    return (responsibility, log_weights, pair_loglik)


def solution(mesh):
    placed = (P(None, "pairs"), P(), P("pairs"), P(), P(), P("comp"), P("comp"), P("comp"))
    return jax.shard_map(
        per_device,
        mesh=mesh,
        in_specs=placed,
        out_specs=(P("comp", "pairs"), P("comp"), P("pairs")),
        check_vma=False,
    )
```

time: 1580 us -> 184 us (0.12)
  other arithmetic: 649 us -> 9.05 us
  waiting for transfers between devices: 404 us -> 0 us
  matrix products: 196 us -> 2.85 us
  local copies, waits for them, and re-layouts: 181 us -> 1.54 us
  Pallas kernels: 0 us -> 129 us
  blocking collectives: 102 us -> 40.8 us
  loops' own time: 31.6 us -> 0 us
    another operation x7 -> x0, other arithmetic: 617 us -> none  [the longest x4 577 us: build_factors(): factor = jnp.linalg.cholesky(system)]
    all_gather x1 -> x0, waiting for transfers between devices: 404 us -> none  [per_device(): lax.all_gather(own_inverse, 'pairs', axis=0, tiled=True)]
    dot_general x22 -> x2, matrix products: 187 us -> 2.85 us  [the longest x1 1.97 us: per_device(): lax.dot_general(covariances.reshape(covariances.shape[0], tissues * padde...]
    pallas_call x0 -> x1, Pallas kernels: none -> 129 us  [score_tiles(): pl.pallas_call(make_body(tissues), grid_spec=grid_spec, out_shape=[jax.Sh...]
    dynamic_slice x48 -> x0, local copies, waits for them, and re-layouts: 85.3 us -> none  [the longest x32 76 us: one_tile(): lax.dynamic_index_in_dim(whiten_table, block_id, 0, keepdims=False)]
    reshape x6 -> x1, local copies, waits for them, and re-layouts: 69.2 us -> 0.18 us  [per_device(): covariances.reshape(covariances.shape[0], tissues * padded)]
    all_gather x3 -> x1, blocking collectives: 63.1 us -> 2.04 us  [per_device(): every = lax.all_gather(part, 'comp')]
    another operation x1 -> x0, loops' own time: 31.6 us -> none  [per_device(): lax.fori_loop(0, local_pairs // TILE, one_tile, jnp.zeros((comp_count, lo...]
  transfers between devices with their start and end apart: 1 -> 0, of which waited for: 1 -> 0; matrix products, arithmetic and copies ran while one was open for 0% -> 0% of each run, Pallas kernels for 0% -> 0%
where the time goes in v1:
time: 184 us
  Pallas kernels  129 us (70%)
  blocking collectives  40.8 us (22%)
  other arithmetic  9.05 us (5%)
  matrix products  2.85 us (2%)
    pallas_call x1, Pallas kernels, score_tiles(): pl.pallas_call(make_body(tissues), grid_spec=grid_spec, out_shape=[jax.Sh...  129 us
    psum x1, blocking collectives, per_device(): masses = lax.psum(jnp.sum(responsibility, axis=1), 'pairs')  38.8 us
    reduce_sum x1, other arithmetic, per_device(): masses = lax.psum(jnp.sum(responsibility, axis=1), 'pairs')  4.76 us

profile of v1, /device:TPU:0, one launch (start us, length us, event | category | flops | bytes accessed | tf_op | source)
XLA Modules:
  0.0 183.8 jit_solution(17754948731649943536)
XLA Ops:
  0.6 0.0 copy-start.1
  0.6 0.0 copy-start
  0.7 0.9 select_reduce_fusion
  1.6 0.9 convert_reduce_fusion
  2.5 0.8 select_reduce_fusion.1
  3.2 0.8 mul.21.se_square
  4.0 1.1 copy.22
  5.2 0.9 convolution_bitcast_fusion
  6.0 0.2 copy.24
  6.3 0.2 reshape.28
  6.5 2.0 %convolution_multiply_fusion = f32[2744,128]{1,0:T(8,128)S(1)} fusion(f32[16,2744]{1,0:T(8,128)S(1)} %reshape.28, f32[128]{0:T(128)S(1)} %mul.22, s32[128]{0:T(128)} %param.13), kind=kOutput, calls=%fused_computation.1 | convolution fusion | flops 67789824 | bytes 1581568 | tf_op jit(solution)/shard_map/dot_general | solution.py:190
  8.4 0.0 copy-done.1
  8.4 0.0 copy-done
  8.4 128.8 %score_tiles.1 = (f32[128,8192]{1,0:T(8,128)}, f32[1,8192]{1,0:T(1,128)S(1)}, f32[1,8192]{1,0:T(1,128)S(1)}) custom-call(s32[16]{0:T(128)S(1)} %get-tuple-element.10.order, s32[16]{0:T(128)S(1)} %get-tuple-element.9.patterns, f32[16,49]{1,0:T(8,128)S(1)} %mul.21.se_square, f32[49,8192]{1,0:T(8,128)S(1)} %copy-done, f32[49,56,128]{2,1,0:T(8,128)S(1)} %bitcast.20, ...), custom_call_target="tpu_custom_call" | custom-call | tf_op jit(solution)/shard_map/score_tiles/pallas_call | solution.py:162
  137.2 0.1 maximum_bitcast_fusion
  137.3 2.0 %all-gather.1 = f32[2,2,8192]{2,1,0:T(2,128)S(1)} all-gather(f32[1,2,8192]{2,1,0:T(2,128)S(1)} %maximum_bitcast_fusion), channel_id=2, replica_groups=mesh['pairs'=16,'comp'=2] {'comp'}, dimensions={0}, use_global_device_ids=true | all-gather | bytes 196608 | tf_op jit(solution)/shard_map/all_gather | solution.py:200
  139.3 0.2 fusion.9
  139.5 0.2 fusion.2
  139.7 0.0 copy-start.2
  139.7 4.8 %fusion.8 = (f32[128]{0:T(128)S(1)}, f32[128,8192]{1,0:T(8,128)}) fusion(f32[128,8192]{1,0:T(8,128)} %get-tuple-element.6, f32[8192]{0:T(1024)S(1)} %log_add_fusion), kind=kLoop, calls=%fused_computation.25 | loop fusion | flops 2097024 | bytes 8421888 | tf_op jit(solution)/shard_map/reduce_sum | solution.py:205
  144.5 0.0 copy-done.2
  144.5 38.8 %psum.7 = f32[128]{0:T(128)S(1)} all-reduce(f32[128]{0:T(128)S(1)} %get-tuple-element.11), channel_id=1, replica_groups=mesh['pairs'=16,'comp'=2] {'pairs'}, use_global_device_ids=true, to_apply=%region_7.8 | all-reduce | flops 128 | bytes 1024 | tf_op jit(solution)/shard_map/psum | solution.py:205
  183.2 0.5 multiply_log_fusion
  (2 shorter events, 0.0 us)
Async XLA Ops:
  0.6 7.8 %copy-start.1 = (f32[128]{0:T(128)S(1)}, f32[128]{0:T(128)}, u32[]{:S(2)}) copy-start(f32[128]{0:T(128)} %param.15) | copy-start | bytes 1540
  0.6 7.8 %copy-start = (f32[49,8192]{1,0:T(8,128)S(1)}, f32[49,8192]{1,0:T(8,128)}, u32[]{:S(2)}) copy-start(f32[49,8192]{1,0:T(8,128)} %effects.1) | copy-start | bytes 4816900
  139.7 4.8 %copy-start.2 = (f32[8192]{0:T(1024)}, f32[8192]{0:T(1024)S(1)}, u32[]{:S(2)}) copy-start(f32[8192]{0:T(1024)S(1)} %log_add_fusion) | copy-start | bytes 98308

commit v2 on v1

--- a/solution.py
+++ b/solution.py
@@ -104,15 +104,14 @@
         wide[slot : slot + tissues, :] = tile - high
         turned = wide[...].T.astype(jnp.bfloat16)
         packed = jnp.concatenate([turned, turned], axis=1)
-        quad[...] = jnp.zeros(quad.shape, quad.dtype)
-
-        def pair_of_rows(index, carry):
+        for index in range(table.shape[0]):
             white = jnp.dot(packed, table[index], preferred_element_type=jnp.float32)
             white = white * white
-            quad[...] += white[:, :comps] + white[:, comps:]
-            return carry
-
-        lax.fori_loop(0, table.shape[0], pair_of_rows, 0)
+            part = white[:, :comps] + white[:, comps:]
+            if index == 0:
+                quad[...] = part
+            else:
+                quad[...] += part
         found = (bias[...] - 0.5 * quad[...]).T
         scores[...] = found
         top = jnp.max(found, axis=0, keepdims=True)
@@ -202,7 +201,9 @@
     score_sum = jnp.sum(every[:, 1] * jnp.exp(every[:, 0] - score_max[None]), axis=0)
     pair_loglik = score_max + jnp.log(score_sum)
     responsibility = jnp.exp(scores - pair_loglik)
-    masses = lax.psum(jnp.sum(responsibility, axis=1), "pairs")
+    own_mass = jnp.sum(responsibility, axis=1)
+    copies = jnp.broadcast_to(own_mass[None], (lax.axis_size("pairs"), comps))
+    masses = jnp.sum(lax.all_to_all(copies, "pairs", 0, 0, tiled=True), axis=0)
     all_pairs = effects.shape[1] * lax.axis_size("pairs")
     all_comps = comps * lax.axis_size("comp")
     log_weights = jnp.log((masses + 1.0) / (all_pairs + all_comps))

time: 184 us -> 93.6 us (0.51)
  Pallas kernels: 129 us -> 60.4 us
  blocking collectives: 40.8 us -> 17.3 us
    pallas_call x1, Pallas kernels: 129 us -> 60.4 us  [score_tiles(): pl.pallas_call(make_body(tissues), grid_spec=grid_spec, out_shape=[jax.Sh...]
    psum x1 -> x0, blocking collectives: 38.8 us -> none  [per_device(): masses = lax.psum(jnp.sum(responsibility, axis=1), 'pairs')]
    all_to_all x0 -> x1, blocking collectives: none -> 15.3 us  [per_device(): masses = jnp.sum(lax.all_to_all(copies, 'pairs', 0, 0, tiled=True), axis=0)]
    reduce_sum x1 -> x2, other arithmetic: 4.76 us -> 4.78 us  [the longest x1 4.76 us: per_device(): own_mass = jnp.sum(responsibility, axis=1)]
where the time goes in v2:
time: 93.6 us; the launch traced here: 91.9 us
  Pallas kernels  60.4 us (65%)
  blocking collectives  17.3 us (18%)
  other arithmetic  9.07 us (10%)
  matrix products  2.85 us (3%)
  local copies, waits for them, and re-layouts  1.55 us (2%)
    pallas_call x1, Pallas kernels, score_tiles(): pl.pallas_call(make_body(tissues), grid_spec=grid_spec, out_shape=[jax.Sh...  60.4 us
    all_to_all x1, blocking collectives, per_device(): masses = jnp.sum(lax.all_to_all(copies, 'pairs', 0, 0, tiled=True), axis=0)  15.3 us
    reduce_sum x1, other arithmetic, per_device(): own_mass = jnp.sum(responsibility, axis=1)  4.76 us
    all_gather x1, blocking collectives, per_device(): every = lax.all_gather(part, 'comp')  2.04 us
    dot_general x1, matrix products, per_device(): lax.dot_general(covariances.reshape(covariances.shape[0], tissues * padde...  1.97 us

profile of v2, /device:TPU:0, one launch (start us, length us, event | category | flops | bytes accessed | tf_op | source)
XLA Modules:
  0.0 91.9 jit_solution(85996169982066072)
XLA Ops:
  0.6 0.0 copy-start.1
  0.6 0.0 copy-start
  0.7 0.9 select_reduce_fusion
  1.6 0.9 convert_reduce_fusion
  2.5 0.8 select_reduce_fusion.1
  3.2 0.8 mul.21.se_square
  4.0 1.1 %copy.26 = f32[16,49,49]{2,1,0:T(8,128)S(1)} copy(f32[16,49,49]{2,0,1:T(8,128)} %param.11) | data formatting | bytes 307328 | tf_op args[3]
  5.2 0.9 convolution_bitcast_fusion
  6.0 0.2 copy.28
  6.3 0.2 reshape.34
  6.5 2.0 %convolution_multiply_fusion = f32[2744,128]{1,0:T(8,128)S(1)} fusion(f32[16,2744]{1,0:T(8,128)S(1)} %reshape.34, f32[128]{0:T(128)S(1)} %mul.22, s32[128]{0:T(128)} %param.13), kind=kOutput, calls=%fused_computation.1 | convolution fusion | flops 67789824 | bytes 1581568 | tf_op jit(solution)/shard_map/dot_general | solution.py:189
  8.4 0.0 copy-done.1
  8.4 0.0 copy-done
  8.4 60.4 %score_tiles.1 = (f32[128,8192]{1,0:T(8,128)}, f32[1,8192]{1,0:T(1,128)S(1)}, f32[1,8192]{1,0:T(1,128)S(1)}) custom-call(s32[16]{0:T(128)S(1)} %get-tuple-element.10.order, s32[16]{0:T(128)S(1)} %get-tuple-element.9.patterns, f32[16,49]{1,0:T(8,128)S(1)} %mul.21.se_square, f32[49,8192]{1,0:T(8,128)S(1)} %copy-done, f32[49,56,128]{2,1,0:T(8,128)S(1)} %bitcast.21, ...), custom_call_target="tpu_custom_call" | custom-call | tf_op jit(solution)/shard_map/score_tiles/pallas_call | solution.py:161
  68.8 0.1 maximum_bitcast_fusion
  68.9 2.0 %all-gather.1 = f32[2,2,8192]{2,1,0:T(2,128)S(1)} all-gather(f32[1,2,8192]{2,1,0:T(2,128)S(1)} %maximum_bitcast_fusion), channel_id=2, replica_groups=mesh['pairs'=16,'comp'=2] {'comp'}, dimensions={0}, use_global_device_ids=true | all-gather | bytes 196608 | tf_op jit(solution)/shard_map/all_gather | solution.py:199
  70.9 0.2 fusion.9
  71.1 0.2 fusion.2
  71.3 0.0 copy-start.2
  71.3 4.8 %fusion.8 = (f32[128]{0:T(128)S(1)}, f32[128,8192]{1,0:T(8,128)}) fusion(f32[128,8192]{1,0:T(8,128)} %get-tuple-element.6, f32[8192]{0:T(1024)S(1)} %log_add_fusion), kind=kLoop, calls=%fused_computation.25 | loop fusion | flops 2097024 | bytes 8421888 | tf_op jit(solution)/shard_map/reduce_sum | solution.py:204
  76.1 0.0 copy-done.2
  76.1 15.3 %all_to_all.6 = f32[16,1,128]{2,1,0:T(1,128)S(1)} all-to-all(f32[16,1,128]{2,1,0:T(1,128)S(1)} %broadcast_in_dim.34), channel_id=1, replica_groups=mesh['pairs'=16,'comp'=2] {'pairs'}, dimensions={0} | all-to-all | bytes 16384 | tf_op jit(solution)/shard_map/all_to_all | solution.py:206
  91.4 0.5 multiply_log_fusion
  (4 shorter events, 0.0 us)
Async XLA Ops:
  0.6 7.8 %copy-start.1 = (f32[128]{0:T(128)S(1)}, f32[128]{0:T(128)}, u32[]{:S(2)}) copy-start(f32[128]{0:T(128)} %param.15) | copy-start | bytes 1540
  0.6 7.8 %copy-start = (f32[49,8192]{1,0:T(8,128)S(1)}, f32[49,8192]{1,0:T(8,128)}, u32[]{:S(2)}) copy-start(f32[49,8192]{1,0:T(8,128)} %effects.1) | copy-start | bytes 4816900
  71.3 4.8 %copy-start.2 = (f32[8192]{0:T(1024)}, f32[8192]{0:T(1024)S(1)}, u32[]{:S(2)}) copy-start(f32[8192]{0:T(1024)S(1)} %log_add_fusion) | copy-start | bytes 98308
